TPU v7x, 128 devices: a whole 4x4x4 slice. The times are simulated.
128 devices in a mesh: ep: 32 (over y, x, core), tp: 4 (over z).
Axes of the slice: x: 4, y: 4, z: 4, core: 2. Of those that a mesh axis runs over, the one named last changes fastest.
Arguments:
- tokens: bfloat16 [8192, 7168], P('ep', 'tp'), may hold values from -78 to 78
- norm_gain: bfloat16 [7168], P('tp'), may hold values from 0.5 to 1.5
- expert_ids: int32 [8192, 8], P('ep'), may hold values from 0 to 255, all different within a row
- gate_prob: bfloat16 [8192, 8], P('ep'), may hold values from 0.049804688 to 1
- w_gate: bfloat16 [32, 7168, 2048], P('ep', None, 'tp'), may hold values from -0.0625 to 0.0625
- w_up: bfloat16 [32, 7168, 2048], P('ep', None, 'tp'), may hold values from -0.0625 to 0.0625
- w_down: bfloat16 [32, 2048, 7168], P('ep', 'tp'), may hold values from -0.125 to 0.125
Outputs:
- combined: bfloat16 [8192, 7168], P('ep', 'tp')
Inputs may be any that keep to these rules, and one draw needn't show every extreme that they name: `expert_ids`: each row names 8 different experts.
All inputs are finite; a program needn't handle non-finite values.
Results may differ from a plain program's by a relative error of at most 0.01.
Values may be sent and summed in bfloat16 or wider, within the bound.
No kernel may reach another device: no remote copies, remote signals or barrier semaphores. Data moves between devices by JAX's collectives and lax.ppermute only.
A program may use at most 128 MiB of HBM per device.

v0:
```python
import jax
import jax.numpy as jnp
from jax import lax
from jax.sharding import PartitionSpec as P

D = 7168
TOP = 8
EXP_DEV = 8
epsilon = 1e-06


def from_everyone(value, axis):
    length = lax.axis_size(axis)
    return lax.all_to_all(
        jnp.broadcast_to(value[None], (length, *value.shape)), axis, 0, 0, tiled=True
    )


def over_copies(value, axis):
    everything = from_everyone(value, axis)
    return jnp.sum(everything, axis=0)


def exchange_in_groups(value, axis, split_dim, concat_dim, work, item_dim, out_dim):
    items = jax.tree.leaves(value)[0].shape[item_dim]
    count = 2 if items % 2 == 0 else 1
    done = []
    for k in range(count):
        group = jax.tree.map(
            lambda a: lax.slice_in_dim(
                a, k * (items // count), (k + 1) * (items // count), axis=item_dim
            ),
            value,
        )
        done.append(
            work(
                lax.all_to_all(
                    group, axis, split_axis=split_dim, concat_axis=concat_dim, tiled=True
                )
            )
        )
    return jax.tree.map(lambda *parts: jnp.concatenate(parts, axis=out_dim), *done)


def place_picks(expert_ids, gate_prob, window, capacity):
    is_live = expert_ids < window
    matches = (expert_ids[:, :, None] == jnp.arange(window, dtype=jnp.int32)).astype(jnp.int32)
    counts = jnp.sum(matches, axis=1)
    before = jnp.cumsum(counts, axis=0) - counts
    slot_index = jnp.sum(matches * before[:, None, :], axis=2)
    is_kept = is_live & (slot_index < capacity)
    target = jnp.where(is_kept, expert_ids * capacity + slot_index, -1)
    hit_table = target[:, :, None] == jnp.arange(window * capacity, dtype=jnp.int32)
    dispatch_mat = jnp.any(hit_table, axis=1).astype(jnp.bfloat16)
    weight_mat = jnp.sum(
        jnp.where(hit_table, gate_prob.astype(jnp.float32)[:, :, None], 0.0), axis=1
    ).astype(jnp.bfloat16)
    return (dispatch_mat, weight_mat)


def run_expert(received, w_gate, w_up, w_down):
    senders, item_count, row_width = received.shape
    flat_rows = received.reshape(senders * item_count, row_width)
    gate_act = jnp.dot(flat_rows, w_gate[0], preferred_element_type=jnp.float32)
    up_act = jnp.dot(flat_rows, w_up[0], preferred_element_type=jnp.float32)
    hidden = (jax.nn.silu(gate_act) * up_act).astype(jnp.bfloat16)
    down_term = jnp.einsum("rf,fc->rc", hidden, w_down[0], preferred_element_type=jnp.float32)
    summed = lax.psum_scatter(down_term.astype(jnp.bfloat16), "tp", scatter_dimension=1, tiled=True)
    shares = summed.reshape(senders, item_count, -1)
    return lax.all_to_all(shares, "ep", split_axis=0, concat_axis=0, tiled=True)


def local(tokens, norm_gain, expert_ids, gate_prob, w_gate, w_up, w_down):
    window = lax.axis_size("ep")
    tok_rows = tokens.shape[0]
    capacity = max(2, 2 * tok_rows * TOP // (EXP_DEV * window))
    dispatch_mat, weight_mat = place_picks(expert_ids, gate_prob, window, capacity)
    values = tokens.astype(jnp.float32)
    square_part = jnp.sum(values * values, axis=1)
    square_total = over_copies(square_part, "tp")
    inverse_rms = lax.rsqrt(square_total / D + epsilon)
    normed = (values * inverse_rms[:, None] * norm_gain.astype(jnp.float32)).astype(jnp.bfloat16)
    outgoing = jnp.einsum("tp,td->pd", dispatch_mat, normed, preferred_element_type=jnp.float32)
    outgoing = outgoing.astype(jnp.bfloat16).reshape(window, capacity, -1)

    def handle(received):
        gathered = lax.all_gather(received, "tp", axis=2, tiled=True)
        return run_expert(gathered, w_gate, w_up, w_down)

    returned = exchange_in_groups(outgoing, "ep", 0, 0, handle, 1, 1)
    flat_back = returned.reshape(-1, returned.shape[2])
    combined = jnp.einsum("tp,pd->td", weight_mat, flat_back, preferred_element_type=jnp.float32)
    return combined.astype(jnp.bfloat16)


def solution(mesh):
    placed = (
        P("ep", "tp"),
        P("tp"),
        P("ep", None),
        P("ep", None),
        P("ep", None, "tp"),
        P("ep", None, "tp"),
        P("ep", "tp", None),
    )
    return jax.shard_map(
        local, mesh=mesh, in_specs=placed, out_specs=P("ep", "tp"), check_vma=False
    )
```

profile of v0, /device:TPU:1, one launch (start us, length us, event | category | flops | bytes accessed | tf_op | source)
XLA Modules:
  0.0 255.4 jit_solution(9727998538408173753)
XLA Ops:
  6.5 1.4 fusion.15
  8.0 0.6 broadcast_in_dim.21
  8.6 5.8 %all-to-all-start = ((f32[4,1,256]{2,1,0:T(1,128)}), f32[4,1,256]{2,1,0:T(1,128)S(1)}, u32[]{:S(2)}, u32[]{:S(2)}) async-start(f32[4,1,256]{2,1,0:T(1,128)} %broadcast_in_dim.21), calls=%async_computation | async-start | bytes 8192 | tf_op jit(solution)/shard_map/all_to_all | solution.py:14
  14.4 0.7 convert_reduce_fusion
  15.2 0.6 reduce-window.6
  15.8 0.2 slice_reduce_fusion
  16.0 0.1 fusion.52
  16.1 0.8 select_reduce_fusion.1
  16.8 0.7 add_select_fusion
  17.5 0.1 copy.23
  17.7 1.7 fusion.10
  19.4 0.7 convert_element_type.41
  20.1 2.0 convolution_convert_fusion.2
  22.1 0.1 fusion.55
  22.3 23.6 %all_to_all.26 = bf16[32,8,1792]{2,1,0:T(8,128)(2,1)} all-to-all(bf16[32,8,1792]{2,1,0:T(8,128)(2,1)S(1)} %get-tuple-element.5), channel_id=1, replica_groups=mesh['ep'=32,'tp'=4] {'ep'}, dimensions={0} | all-to-all | bytes 1835008 | tf_op jit(solution)/shard_map/all_to_all | solution.py:37
  45.9 19.5 %all_to_all.27 = bf16[32,8,1792]{2,1,0:T(8,128)(2,1)} all-to-all(bf16[32,8,1792]{2,1,0:T(8,128)(2,1)S(1)} %get-tuple-element.6), channel_id=1, replica_groups=mesh['ep'=32,'tp'=4] {'ep'}, dimensions={0} | all-to-all | bytes 1835008 | tf_op jit(solution)/shard_map/all_to_all | solution.py:37
  65.5 22.4 %all-gather.3.cloned.1.call-done = bf16[32,8,7168]{2,1,0:T(8,128)(2,1)} async-done(((bf16[32,8,1792]{2,1,0:T(8,128)(2,1)}), bf16[32,8,7168]{2,1,0:T(8,128)(2,1)}) %all-gather.3.cloned.1.call-update) | async-done | bytes 3670032 | tf_op jit(solution)/shard_map/all_gather | solution.py:87
  87.9 6.2 %fusion.8 = f32[256,512]{1,0:T(8,128)S(1)} fusion(bf16[1,7168,512]{2,1,0:T(8,128)(2,1)} %param.11, bf16[32,8,7168]{2,1,0:T(8,128)(2,1)} %all-gather.3.cloned.1.call-done), kind=kOutput, calls=%fused_computation.10 | convolution fusion | flops 1879048192 | bytes 11534336 | tf_op jit(solution)/shard_map/dot_general | solution.py:64
  94.1 12.6 %convolution_convert_fusion.1 = bf16[256,7168]{1,0:T(8,128)(2,1)} fusion(bf16[1,512,7168]{2,1,0:T(8,128)(2,1)} %param.13, bf16[1,7168,512]{2,1,0:T(8,128)(2,1)} %param.12, bf16[32,8,7168]{2,1,0:T(8,128)(2,1)} %all-gather.3.cloned.1.call-done, f32[256,512]{1,0:T(8,128)S(1)} %fusion.8), kind=kOutput, calls=%fused_computation.1 | convolution fusion | flops 3760717824 | bytes 22544384 | tf_op jit(solution)/shard_map/rf,fc->rc/dot_general | solution.py:67
  106.8 0.2 reduce-scatter.5.cloned.1.call-start
  107.0 26.7 %all-gather.5.cloned.1.call-done = bf16[32,8,7168]{2,1,0:T(8,128)(2,1)} async-done(((bf16[32,8,1792]{2,1,0:T(8,128)(2,1)}), bf16[32,8,7168]{2,1,0:T(8,128)(2,1)}) %all-gather.5.cloned.1.call-update) | async-done | bytes 3670032 | tf_op jit(solution)/shard_map/all_gather | solution.py:87
  133.8 6.2 %fusion.6 = f32[256,512]{1,0:T(8,128)S(1)} fusion(bf16[1,7168,512]{2,1,0:T(8,128)(2,1)} %param.11, bf16[32,8,7168]{2,1,0:T(8,128)(2,1)} %all-gather.5.cloned.1.call-done), kind=kOutput, calls=%fused_computation.8 | convolution fusion | flops 1879048192 | bytes 11534336 | tf_op jit(solution)/shard_map/dot_general | solution.py:64
  140.0 12.8 %convolution_convert_fusion = bf16[256,7168]{1,0:T(8,128)(2,1)} fusion(bf16[1,512,7168]{2,1,0:T(8,128)(2,1)} %param.13, bf16[1,7168,512]{2,1,0:T(8,128)(2,1)} %param.12, bf16[32,8,7168]{2,1,0:T(8,128)(2,1)} %all-gather.5.cloned.1.call-done, f32[256,512]{1,0:T(8,128)S(1)} %fusion.6), kind=kOutput, calls=%fused_computation | convolution fusion | flops 3760717824 | bytes 22544384 | tf_op jit(solution)/shard_map/rf,fc->rc/dot_general | solution.py:67
  152.9 26.3 %reduce-scatter.3.cloned.1.call-done = bf16[256,1792]{1,0:T(8,128)(2,1)} async-done(((bf16[256,7168]{1,0:T(8,128)(2,1)}), bf16[256,1792]{1,0:T(8,128)(2,1)}) %reduce-scatter.3.cloned.1.call-update) | async-done | bytes 917520 | tf_op jit(solution)/shard_map/reduce_scatter | solution.py:68
  179.2 7.6 %all-to-all-start.2 = ((bf16[32,8,1792]{2,1,0:T(8,128)(2,1)}), bf16[32,8,1792]{2,1,0:T(8,128)(2,1)S(1)}, u32[]{:S(2)}, u32[]{:S(2)}) async-start(bf16[32,8,1792]{2,1,0:T(8,128)(2,1)} %bitcast.75), calls=%async_computation.3 | async-start | bytes 1835008 | tf_op jit(solution)/shard_map/all_to_all | solution.py:70
  186.8 37.1 %reduce-scatter.5.cloned.1.call-done = bf16[256,1792]{1,0:T(8,128)(2,1)} async-done(((bf16[256,7168]{1,0:T(8,128)(2,1)}), bf16[256,1792]{1,0:T(8,128)(2,1)}) %reduce-scatter.5.cloned.1.call-update) | async-done | bytes 917520 | tf_op jit(solution)/shard_map/reduce_scatter | solution.py:68
  223.9 7.6 %all-to-all-start.4 = ((bf16[32,8,1792]{2,1,0:T(8,128)(2,1)}), bf16[32,8,1792]{2,1,0:T(8,128)(2,1)S(1)}, u32[]{:S(2)}, u32[]{:S(2)}) async-start(bf16[32,8,1792]{2,1,0:T(8,128)(2,1)} %bitcast.76), calls=%async_computation.6 | async-start | bytes 1835008 | tf_op jit(solution)/shard_map/all_to_all | solution.py:70
  231.5 0.1 copy.24
  231.6 1.7 select_reduce_fusion
  233.3 13.8 %all-to-all-done.4 = bf16[32,8,1792]{2,1,0:T(8,128)(2,1)S(1)} async-done(((bf16[32,8,1792]{2,1,0:T(8,128)(2,1)}), bf16[32,8,1792]{2,1,0:T(8,128)(2,1)S(1)}, u32[]{:S(2)}, u32[]{:S(2)}) %all-to-all-start.4) | async-done | bytes 917536 | tf_op jit(solution)/shard_map/all_to_all | solution.py:70
  247.1 0.1 pad_maximum_fusion
  247.3 1.6 convolution_convert_fusion.3
  (16 shorter events, 0.2 us)
Async XLA Ops:
  8.6 11.5 %all-to-all-start = ((f32[4,1,256]{2,1,0:T(1,128)}), f32[4,1,256]{2,1,0:T(1,128)S(1)}, u32[]{:S(2)}, u32[]{:S(2)}) async-start(f32[4,1,256]{2,1,0:T(1,128)} %broadcast_in_dim.21), calls=%async_computation | async-start | bytes 8192 | tf_op jit(solution)/shard_map/all_to_all | solution.py:14
  14.4 73.5 %all-gather.3.cloned.1.call-start = ((), (), s32[]{:S(2)}) async-start(), calls=%async_computation.7 | async-start | bytes 4587520 | tf_op jit(solution)/shard_map/all_gather | solution.py:87
  45.9 87.9 %all-gather.5.cloned.1.call-start = ((), (), s32[]{:S(2)}) async-start(), calls=%async_computation.9 | async-start | bytes 4587520 | tf_op jit(solution)/shard_map/all_gather | solution.py:87
  65.5 113.8 %reduce-scatter.3.cloned.1.call-start = ((), (), s32[]{:S(2)}) async-start(), calls=%async_computation.8 | async-start | bytes 4587520 | tf_op jit(solution)/shard_map/reduce_scatter | solution.py:68
  106.8 117.1 %reduce-scatter.5.cloned.1.call-start = ((), (), s32[]{:S(2)}) async-start(), calls=%async_computation.10 | async-start | bytes 4587520 | tf_op jit(solution)/shard_map/reduce_scatter | solution.py:68
  152.8 78.6 %copy-start = (bf16[256,8]{0,1:T(8,128)(2,1)S(1)}, bf16[256,8]{0,1:T(8,128)(2,1)}, u32[]{:S(2)}) copy-start(bf16[256,8]{0,1:T(8,128)(2,1)} %param.10) | copy-start | bytes 12292
  179.2 44.7 %all-to-all-start.2 = ((bf16[32,8,1792]{2,1,0:T(8,128)(2,1)}), bf16[32,8,1792]{2,1,0:T(8,128)(2,1)S(1)}, u32[]{:S(2)}, u32[]{:S(2)}) async-start(bf16[32,8,1792]{2,1,0:T(8,128)(2,1)} %bitcast.75), calls=%async_computation.3 | async-start | bytes 1835008 | tf_op jit(solution)/shard_map/all_to_all | solution.py:70
  223.9 23.2 %all-to-all-start.4 = ((bf16[32,8,1792]{2,1,0:T(8,128)(2,1)}), bf16[32,8,1792]{2,1,0:T(8,128)(2,1)S(1)}, u32[]{:S(2)}, u32[]{:S(2)}) async-start(bf16[32,8,1792]{2,1,0:T(8,128)(2,1)} %bitcast.76), calls=%async_computation.6 | async-start | bytes 1835008 | tf_op jit(solution)/shard_map/all_to_all | solution.py:70
Sparse Core Ops, SparseCore 0:
  46.0 41.8 all-gather.2
  89.6 44.1 all-gather.4
  136.2 42.9 reduce-scatter.2
  181.5 42.3 reduce-scatter.4
where the time goes:
time: 256 us; the launch traced here: 255 us
  waiting for transfers between devices  126 us (49%)
  blocking collectives  43.1 us (17%)
  matrix products  41.6 us (16%)
  starting transfers between devices  21.3 us (8%)
  between operations  13.2 us (5%)
  other arithmetic  8.58 us (3%)
    reduce_scatter x2, waiting for transfers between devices, run_expert(): lax.psum_scatter(down_term.astype(jnp.bfloat16), 'tp', scatter_dimension=...  63.4 us
    all_gather x2, waiting for transfers between devices, handle(): gathered = lax.all_gather(received, 'tp', axis=2, tiled=True)  49.1 us
    all_to_all x2, blocking collectives, exchange_in_groups(): lax.all_to_all(group, axis, split_axis=split_dim, concat_axis=concat_dim,...  43.1 us
    dot_general x2, matrix products, run_expert(): jnp.einsum('rf,fc->rc', hidden, w_down[0], preferred_element_type=jnp.flo...  25.5 us
    all_to_all x2, starting transfers between devices, run_expert(): return lax.all_to_all(shares, 'ep', split_axis=0, concat_axis=0, tiled=True)  15.2 us
    all_to_all x2, waiting for transfers between devices, run_expert(): return lax.all_to_all(shares, 'ep', split_axis=0, concat_axis=0, tiled=True)  13.8 us
    dot_general x2, matrix products, run_expert(): gate_act = jnp.dot(flat_rows, w_gate[0], preferred_element_type=jnp.float32)  12.5 us
    all_to_all x1, starting transfers between devices, from_everyone(): lax.all_to_all(jnp.broadcast_to(value[None], (length, *value.shape)), axi...  5.84 us
  transfers between devices with their start and end apart: 7, of which 5 were waited for; matrix products, arithmetic and copies ran while one was open for 18% of the time, Pallas kernels for 0%

commit v1 on v0

--- a/solution.py
+++ b/solution.py
@@ -84,7 +84,10 @@
     outgoing = outgoing.astype(jnp.bfloat16).reshape(window, capacity, -1)
 
     def handle(received):
-        gathered = lax.all_gather(received, "tp", axis=2, tiled=True)
+        size = lax.axis_size("tp")
+        pieces = jnp.stack([received for _ in range(size)])
+        pieces = lax.all_to_all(pieces, "tp", split_axis=0, concat_axis=0)
+        gathered = jnp.concatenate(pieces, axis=2)
         return run_expert(gathered, w_gate, w_up, w_down)
 
     returned = exchange_in_groups(outgoing, "ep", 0, 0, handle, 1, 1)

time: 256 us -> 285 us (1.11)
  blocking collectives: 43.1 us -> 148 us
  waiting for transfers between devices: 126 us -> 48.4 us
  local copies, waits for them, and re-layouts: 1.14 us -> 12.3 us
  matrix products: 41.6 us -> 32 us
    all_to_all x0 -> x2, blocking collectives: none -> 104 us  [handle(): pieces = lax.all_to_all(pieces, 'tp', split_axis=0, concat_axis=0)]
    all_gather x2 -> x0, waiting for transfers between devices: 49.1 us -> none  [handle(): gathered = lax.all_gather(received, 'tp', axis=2, tiled=True)]
    reduce_scatter x2, waiting for transfers between devices: 63.4 us -> 34.5 us  [run_expert(): lax.psum_scatter(down_term.astype(jnp.bfloat16), 'tp', scatter_dimension=...]
    dot_general x2, matrix products: 12.5 us -> 4.28 us  [run_expert(): gate_act = jnp.dot(flat_rows, w_gate[0], preferred_element_type=jnp.float32)]
    reshape x1 -> x3, local copies, waits for them, and re-layouts: 0.01 us -> 5.67 us  [the longest x2 5.67 us: handle(): gathered = jnp.concatenate(pieces, axis=2)]
    unnamed x2 -> x16, local copies, waits for them, and re-layouts: 0.01 us -> 5.07 us
  transfers between devices with their start and end apart: 7 -> 5, of which waited for: 5 -> 2; matrix products, arithmetic and copies ran while one was open for 18% -> 9% of each run, Pallas kernels for 0% -> 0%
where the time goes in v1:
time: 285 us; the launch traced here: 284 us
  blocking collectives  148 us (52%)
  waiting for transfers between devices  48.4 us (17%)
  matrix products  32 us (11%)
  starting transfers between devices  21 us (7%)
  between operations  13.6 us (5%)
  local copies, waits for them, and re-layouts  12.3 us (4%)
  other arithmetic  8.58 us (3%)
    all_to_all x2, blocking collectives, handle(): pieces = lax.all_to_all(pieces, 'tp', split_axis=0, concat_axis=0)  104 us
    all_to_all x2, blocking collectives, exchange_in_groups(): lax.all_to_all(group, axis, split_axis=split_dim, concat_axis=concat_dim,...  44.5 us
    reduce_scatter x2, waiting for transfers between devices, run_expert(): lax.psum_scatter(down_term.astype(jnp.bfloat16), 'tp', scatter_dimension=...  34.5 us
    dot_general x2, matrix products, run_expert(): jnp.einsum('rf,fc->rc', hidden, w_down[0], preferred_element_type=jnp.flo...  24.2 us
    all_to_all x2, starting transfers between devices, run_expert(): return lax.all_to_all(shares, 'ep', split_axis=0, concat_axis=0, tiled=True)  15.1 us
    all_to_all x2, waiting for transfers between devices, run_expert(): return lax.all_to_all(shares, 'ep', split_axis=0, concat_axis=0, tiled=True)  13.8 us
    all_to_all x1, starting transfers between devices, from_everyone(): lax.all_to_all(jnp.broadcast_to(value[None], (length, *value.shape)), axi...  5.84 us
  transfers between devices with their start and end apart: 5, of which 2 were waited for; matrix products, arithmetic and copies ran while one was open for 9% of the time, Pallas kernels for 0%

profile of v1, /device:TPU:1, one launch (start us, length us, event | category | flops | bytes accessed | tf_op | source)
XLA Modules:
  0.0 284.4 jit_solution(3998032185391487300)
XLA Ops:
  6.5 1.4 fusion.11
  8.0 0.6 broadcast_in_dim.21
  8.6 5.8 %all-to-all-start = ((f32[4,1,256]{2,1,0:T(1,128)}), f32[4,1,256]{2,1,0:T(1,128)S(1)}, u32[]{:S(2)}, u32[]{:S(2)}) async-start(f32[4,1,256]{2,1,0:T(1,128)} %broadcast_in_dim.21), calls=%async_computation | async-start | bytes 8192 | tf_op jit(solution)/shard_map/all_to_all | solution.py:14
  14.4 0.7 convert_reduce_fusion
  15.2 0.6 reduce-window.6
  16.1 0.8 select_reduce_fusion.1
  16.8 0.7 add_select_fusion
  17.7 1.7 fusion.10
  19.4 0.7 convert_element_type.41
  20.1 2.0 convolution_convert_fusion.2
  22.2 23.5 %all_to_all.36 = bf16[32,8,1792]{2,1,0:T(8,128)(2,1)S(1)} all-to-all(bf16[32,8,1792]{2,1,0:T(8,128)(2,1)S(1)} %get-tuple-element.5), channel_id=1, replica_groups=mesh['ep'=32,'tp'=4] {'ep'}, dimensions={0} | all-to-all | bytes 1835008 | tf_op jit(solution)/shard_map/all_to_all | solution.py:37
  45.7 0.2 stack.4
  46.0 46.9 %all_to_all.37 = bf16[4,32,8,1792]{3,2,1,0:T(8,128)(2,1)S(1)} all-to-all(bf16[4,32,8,1792]{3,2,1,0:T(8,128)(2,1)S(1)} %stack.4), channel_id=1, replica_groups=mesh['ep'=32,'tp'=4] {'tp'}, dimensions={0} | all-to-all | bytes 7340032 | tf_op jit(solution)/shard_map/all_to_all | solution.py:89
  92.8 2.8 copy.48
  95.7 0.7 copy.41
  96.4 1.8 copy-done
  98.2 2.1 fusion.8
  100.3 12.1 %convolution_convert_fusion.1 = bf16[256,7168]{1,0:T(8,128)(2,1)} fusion(bf16[1,512,7168]{2,1,0:T(8,128)(2,1)} %param.13, bf16[256,7168]{1,0:T(8,128)(2,1)} %bitcast.72, bf16[1,7168,512]{2,1,0:T(8,128)(2,1)} %param.12, f32[256,512]{1,0:T(8,128)S(1)} %fusion.8), kind=kOutput, calls=%fused_computation.1 | convolution fusion | flops 3760717824 | bytes 22544384 | tf_op jit(solution)/shard_map/rf,fc->rc/dot_general | solution.py:67
  112.5 21.0 %all_to_all.38 = bf16[32,8,1792]{2,1,0:T(8,128)(2,1)S(1)} all-to-all(bf16[32,8,1792]{2,1,0:T(8,128)(2,1)S(1)} %get-tuple-element.6), channel_id=1, replica_groups=mesh['ep'=32,'tp'=4] {'ep'}, dimensions={0} | all-to-all | bytes 1835008 | tf_op jit(solution)/shard_map/all_to_all | solution.py:37
  133.5 0.2 stack.5
  133.7 57.1 %all_to_all.39 = bf16[4,32,8,1792]{3,2,1,0:T(8,128)(2,1)S(1)} all-to-all(bf16[4,32,8,1792]{3,2,1,0:T(8,128)(2,1)S(1)} %stack.5), channel_id=1, replica_groups=mesh['ep'=32,'tp'=4] {'tp'}, dimensions={0} | all-to-all | bytes 7340032 | tf_op jit(solution)/shard_map/all_to_all | solution.py:89
  190.9 2.8 copy.47
  193.7 0.7 copy.42
  194.4 1.9 copy-done.1
  196.3 2.1 fusion.6
  198.4 12.1 %convolution_convert_fusion = bf16[256,7168]{1,0:T(8,128)(2,1)} fusion(bf16[1,512,7168]{2,1,0:T(8,128)(2,1)} %param.13, bf16[256,7168]{1,0:T(8,128)(2,1)} %bitcast.74, bf16[1,7168,512]{2,1,0:T(8,128)(2,1)} %param.12, f32[256,512]{1,0:T(8,128)S(1)} %fusion.6), kind=kOutput, calls=%fused_computation | convolution fusion | flops 3760717824 | bytes 22544384 | tf_op jit(solution)/shard_map/rf,fc->rc/dot_general | solution.py:67
  210.6 7.5 %all-to-all-start.3 = ((bf16[32,8,1792]{2,1,0:T(8,128)(2,1)}), bf16[32,8,1792]{2,1,0:T(8,128)(2,1)S(1)}, u32[]{:S(2)}, u32[]{:S(2)}) async-start(bf16[32,8,1792]{2,1,0:T(8,128)(2,1)} %bitcast.75), calls=%async_computation.4 | async-start | bytes 1835008 | tf_op jit(solution)/shard_map/all_to_all | solution.py:70
  218.1 34.5 %reduce-scatter.5.cloned.1.call-done = bf16[256,1792]{1,0:T(8,128)(2,1)} async-done(((bf16[256,7168]{1,0:T(8,128)(2,1)}), bf16[256,1792]{1,0:T(8,128)(2,1)}) %reduce-scatter.5.cloned.1.call-update) | async-done | bytes 917520 | tf_op jit(solution)/shard_map/reduce_scatter | solution.py:68
  252.6 7.6 %all-to-all-start.6 = ((bf16[32,8,1792]{2,1,0:T(8,128)(2,1)}), bf16[32,8,1792]{2,1,0:T(8,128)(2,1)S(1)}, u32[]{:S(2)}, u32[]{:S(2)}) async-start(bf16[32,8,1792]{2,1,0:T(8,128)(2,1)} %bitcast.76), calls=%async_computation.8 | async-start | bytes 1835008 | tf_op jit(solution)/shard_map/all_to_all | solution.py:70
  260.3 1.7 select_reduce_fusion
  262.0 13.8 %all-to-all-done.6 = bf16[32,8,1792]{2,1,0:T(8,128)(2,1)S(1)} async-done(((bf16[32,8,1792]{2,1,0:T(8,128)(2,1)}), bf16[32,8,1792]{2,1,0:T(8,128)(2,1)S(1)}, u32[]{:S(2)}, u32[]{:S(2)}) %all-to-all-start.6) | async-done | bytes 917536 | tf_op jit(solution)/shard_map/all_to_all | solution.py:70
  276.0 1.6 convolution_convert_fusion.3
  (32 shorter events, 0.9 us)
Async XLA Ops:
  8.6 11.5 %all-to-all-start = ((f32[4,1,256]{2,1,0:T(1,128)}), f32[4,1,256]{2,1,0:T(1,128)S(1)}, u32[]{:S(2)}, u32[]{:S(2)}) async-start(f32[4,1,256]{2,1,0:T(1,128)} %broadcast_in_dim.21), calls=%async_computation | async-start | bytes 8192 | tf_op jit(solution)/shard_map/all_to_all | solution.py:14
  14.4 196.2 %reduce-scatter.3.cloned.1.call-start = ((), (), s32[]{:S(2)}) async-start(), calls=%async_computation.9 | async-start | bytes 4587520 | tf_op jit(solution)/shard_map/reduce_scatter | solution.py:68
  46.0 52.2 %slice-start = ((s8[7340032]{0:T(1024)(128)(4,1)}), s8[4194304]{0:T(1024)(128)(4,1)S(1)}, s32[]{:S(2)}) async-start(s8[7340032]{0:T(1024)(128)(4,1)} %bitcast.77), calls=%async_computation.11 | async-start | bytes 8388608
  92.8 5.3 %slice-start.1 = ((s8[7340032]{0:T(1024)(128)(4,1)}), s8[3145728]{0:T(1024)(128)(4,1)S(1)}, s32[]{:S(2)}) async-start(s8[7340032]{0:T(1024)(128)(4,1)} %bitcast.77), calls=%async_computation.12 | async-start | bytes 6291456
  96.3 1.8 copy-start
  112.4 140.2 %reduce-scatter.5.cloned.1.call-start = ((), (), s32[]{:S(2)}) async-start(), calls=%async_computation.10 | async-start | bytes 4587520 | tf_op jit(solution)/shard_map/reduce_scatter | solution.py:68
  133.7 62.5 %slice-start.2 = ((s8[7340032]{0:T(1024)(128)(4,1)}), s8[4194304]{0:T(1024)(128)(4,1)S(1)}, s32[]{:S(2)}) async-start(s8[7340032]{0:T(1024)(128)(4,1)} %bitcast.79), calls=%async_computation.13 | async-start | bytes 8388608
  190.9 5.4 %slice-start.3 = ((s8[7340032]{0:T(1024)(128)(4,1)}), s8[3145728]{0:T(1024)(128)(4,1)S(1)}, s32[]{:S(2)}) async-start(s8[7340032]{0:T(1024)(128)(4,1)} %bitcast.79), calls=%async_computation.14 | async-start | bytes 6291456
  194.4 1.9 copy-start.1
  210.5 49.7 %copy-start.2 = (bf16[256,8]{0,1:T(8,128)(2,1)S(1)}, bf16[256,8]{0,1:T(8,128)(2,1)}, u32[]{:S(2)}) copy-start(bf16[256,8]{0,1:T(8,128)(2,1)} %param.10) | copy-start | bytes 12292
  210.6 42.0 %all-to-all-start.3 = ((bf16[32,8,1792]{2,1,0:T(8,128)(2,1)}), bf16[32,8,1792]{2,1,0:T(8,128)(2,1)S(1)}, u32[]{:S(2)}, u32[]{:S(2)}) async-start(bf16[32,8,1792]{2,1,0:T(8,128)(2,1)} %bitcast.75), calls=%async_computation.4 | async-start | bytes 1835008 | tf_op jit(solution)/shard_map/all_to_all | solution.py:70
  252.6 23.3 %all-to-all-start.6 = ((bf16[32,8,1792]{2,1,0:T(8,128)(2,1)}), bf16[32,8,1792]{2,1,0:T(8,128)(2,1)S(1)}, u32[]{:S(2)}, u32[]{:S(2)}) async-start(bf16[32,8,1792]{2,1,0:T(8,128)(2,1)} %bitcast.76), calls=%async_computation.8 | async-start | bytes 1835008 | tf_op jit(solution)/shard_map/all_to_all | solution.py:70
Sparse Core Ops, SparseCore 0:
  112.5 59.4 reduce-scatter.2
  210.7 41.8 reduce-scatter.4
